TPU v7x, 32 devices: a 4x4x1 block of a 4x4x8 slice. The times are simulated.
32 devices in a mesh: dp: 2 (over z, core), tp: 16 (over x, y).
Axes of the slice: x: 4, y: 4, z: 1, core: 2. Of those that a mesh axis runs over, the one named last changes fastest.
The devices are a block of a 4x4x8 slice.
Arguments:
- x: bfloat16 [128, 3072], P('dp'), parts along dimension 0
- k_cache: bfloat16 [128, 2048, 32, 96], P('dp', None, 'tp'), parts along dimension 0
- v_cache: bfloat16 [128, 2048, 32, 96], P('dp', None, 'tp'), parts along dimension 0
- gain_a: bfloat16 [3072], replicated
- wq: bfloat16 [3072, 3072], P(None, 'tp')
- wo: bfloat16 [3072, 3072], P('tp')
- gain_m: bfloat16 [3072], replicated
- w_gate: bfloat16 [3072, 8192], P(None, 'tp')
- w_up: bfloat16 [3072, 8192], P(None, 'tp')
- w_down: bfloat16 [8192, 3072], P('tp')
Outputs:
- output: bfloat16 [128, 3072], P('dp'), parts along dimension 0
There are 2 independent parts. A program takes and returns all parts, laid end to end along the dimension named above; an argument that names none is the same for every part.
All inputs are finite; a program needn't handle non-finite values.
Results may differ from a plain program's by a relative error of at most 0.017.
Values are sent between devices in bfloat16 or wider.
A program may use at most 768 MiB of HBM per device.

v0:
```python
import jax
import jax.numpy as jnp
from jax import lax
from jax.sharding import PartitionSpec as P

HEAD = 96
THETA = 10000


def normed(x, gain):
    wide = x.astype(jnp.float32)
    scale = lax.rsqrt(jnp.mean(wide * wide, -1, keepdims=True) + 1e-6)
    return (wide * scale * gain.astype(jnp.float32)).astype(jnp.bfloat16)


def turned(t, place, theta):
    half = t.shape[-1] // 2
    angle = place.astype(jnp.float32)[:, None] * theta ** (-jnp.arange(half, dtype=jnp.float32) / half)
    cos, sin = jnp.cos(angle)[:, None], jnp.sin(angle)[:, None]
    a, b = t[..., :half].astype(jnp.float32), t[..., half:].astype(jnp.float32)
    return jnp.concatenate([a * cos - b * sin, b * cos + a * sin], -1).astype(jnp.bfloat16)


def matmul(a, w):
    return jnp.dot(a, w, preferred_element_type=jnp.float32).astype(jnp.bfloat16)


def einsum(form, a, b):
    return jnp.einsum(form, a.astype(jnp.float32), b.astype(jnp.float32))


def seen_by(a, wq, k_cache, v_cache, head, theta):
    batch, cache, kv_heads = k_cache.shape[:3]
    place = jnp.full((batch,), cache - 1)
    q = turned(matmul(a, wq).reshape(batch, -1, head), place, theta).reshape(batch, kv_heads, -1, head)
    scores = einsum("bgsd,bugd->bgsu", q, k_cache) * head**-0.5
    weights = jax.nn.softmax(scores, -1).astype(jnp.bfloat16)
    return einsum("bgsu,bugd->bgsd", weights, v_cache).astype(jnp.bfloat16).reshape(batch, -1)


def hidden_of(b, w_gate, w_up):
    gate = jnp.dot(b, w_gate, preferred_element_type=jnp.float32)
    up = jnp.dot(b, w_up, preferred_element_type=jnp.float32)
    return (jax.nn.silu(gate) * up).astype(jnp.bfloat16)


def solution(mesh):
    def added(t, term):
        return (t.astype(jnp.float32) + lax.psum(term.astype(jnp.bfloat16), "tp").astype(jnp.float32)).astype(jnp.bfloat16)

    def step(x, k_cache, v_cache, gain_a, wq, wo, gain_m, w_gate, w_up, w_down):
        seen = seen_by(normed(x, gain_a), wq, k_cache, v_cache, HEAD, THETA)
        h = added(x, jnp.dot(seen, wo, preferred_element_type=jnp.float32))
        return added(h, jnp.dot(hidden_of(normed(h, gain_m), w_gate, w_up), w_down, preferred_element_type=jnp.float32))

    states, cache, columns, rows_of = P("dp", None), P("dp", None, "tp", None), P(None, "tp"), P("tp", None)
    return jax.shard_map(
        step,
        mesh=mesh,
        in_specs=(states, cache, cache, P(None), columns, rows_of, P(None), columns, columns, rows_of),
        out_specs=states,
        check_vma=False,
    )
```

profile of v0, /device:TPU:96, one launch (start us, length us, event | category | flops | bytes accessed | tf_op | source)
XLA Modules:
  0.0 225.5 jit_solution(2986706222907834728)
XLA Ops:
  6.5 0.0 copy-start
  6.6 0.0 all-reduce.3.cloned.1.call-start
  6.6 0.8 convert_element_type.66
  7.5 1.2 fusion.11
  8.7 1.9 convolution_convert_fusion.2
  10.6 0.1 copy.11
  10.8 0.1 fusion.34
  10.9 0.1 copy.12
  11.0 19.7 %fusion.45 = f32[64,2,1,2048]{3,2,1,0:T(1,128)} fusion(bf16[64,2,96,1]{2,3,1,0:T(2,128)(2,1)S(1)} %copy.12, bf16[64,2048,2,96]{1,3,2,0:T(8,128)(2,1)} %param.11), kind=kOutput, calls=%fused_computation.58 | convolution fusion | flops 50331648 | bytes 51404800 | tf_op jit(solution)/shard_map/bgsd,bugd->bgsu/dot_general | solution.py:29
  30.7 3.4 %fusion.6 = bf16[64,2,2048,1]{2,0,1,3:T(8,128)(2,1)} fusion(f32[64,2,1,2048]{3,2,1,0:T(1,128)} %fusion.45), kind=kOutput, calls=%fused_computation.8 | output fusion | flops 1052926 | bytes 1572864 | tf_op jit(solution)/shard_map/div | solution.py:37
  34.1 19.9 %fusion.8 = f32[64,2,1,96]{3,2,1,0:T(1,128)S(1)} fusion(bf16[64,2048,2,96]{1,3,2,0:T(8,128)(2,1)} %param.12, bf16[64,2,2048,1]{2,0,1,3:T(8,128)(2,1)} %fusion.6), kind=kOutput, calls=%fused_computation.19 | convolution fusion | flops 50331648 | bytes 50905088 | tf_op jit(solution)/shard_map/bgsu,bugd->bgsd/dot_general | solution.py:29
  54.0 0.1 reshape.62
  54.1 2.4 %convolution_convert_fusion.1 = bf16[64,3072]{1,0:T(8,128)(2,1)} fusion(bf16[64,192]{1,0:T(8,128)(2,1)S(1)} %reshape.62, bf16[192,3072]{1,0:T(8,128)(2,1)} %param.15), kind=kOutput, calls=%fused_computation.3 | convolution fusion | flops 75694080 | bytes 1597440 | tf_op jit(solution)/shard_map/dot_general | solution.py:53
  56.5 0.1 all-reduce.3.cloned.1.call-update
  56.5 0.1 all-reduce.5.cloned.1.call-start
  56.6 0.0 copy-done.1
  56.6 77.3 %all-reduce.3.cloned.1.call-done = bf16[64,3072]{1,0:T(8,128)(2,1)} async-done(((bf16[64,3072]{1,0:T(8,128)(2,1)}), bf16[64,3072]{1,0:T(8,128)(2,1)}) %all-reduce.3.cloned.1.call-update) | async-done | bytes 393232 | tf_op jit(solution)/shard_map/psum | solution.py:49
  134.0 1.4 fusion.15
  135.3 3.2 %fusion.30 = f32[64,512]{1,0:T(8,128)} fusion(bf16[3072,512]{1,0:T(8,128)(2,1)} %param.17, bf16[64,3072]{1,0:T(8,128)(2,1)S(1)} %get-tuple-element.6, f32[3072]{0:T(1024)S(1)} %convert_element_type.77, f32[64]{0:T(128)S(1)} %add_rsqrt_fusion), kind=kOutput, calls=%fused_computation.38 | convolution fusion | flops 202113024 | bytes 3682560 | tf_op jit(solution)/shard_map/dot_general | solution.py:42
  138.6 0.0 copy-done
  138.6 4.0 %convolution_convert_fusion = bf16[64,3072]{1,0:T(8,128)(2,1)} fusion(bf16[512,3072]{1,0:T(8,128)(2,1)S(1)} %copy-done, bf16[3072,512]{1,0:T(8,128)(2,1)} %param.18, f32[64,512]{1,0:T(8,128)} %fusion.30, bf16[64,3072]{1,0:T(8,128)(2,1)S(1)} %get-tuple-element.6, f32[3072]{0:T(1024)S(1)} %convert_element_type.77, f32[64]{0:T(128)S(1)} %add_rsqrt_fusion), kind=kOutput, calls=%fused_computation.2 | convolution fusion | flops 403832832 | bytes 7221504 | tf_op jit(solution)/shard_map/dot_general | solution.py:54
  142.5 0.1 all-reduce.5.cloned.1.call-update
  142.6 74.2 %all-reduce.5.cloned.1.call-done = bf16[64,3072]{1,0:T(8,128)(2,1)} async-done(((bf16[64,3072]{1,0:T(8,128)(2,1)}), bf16[64,3072]{1,0:T(8,128)(2,1)}) %all-reduce.5.cloned.1.call-update) | async-done | bytes 393232 | tf_op jit(solution)/shard_map/psum | solution.py:49
  216.8 1.8 fusion.18
  (7 shorter events, 0.1 us)
Async XLA Ops:
  6.5 132.0 %copy-start = (bf16[512,3072]{1,0:T(8,128)(2,1)S(1)}, bf16[512,3072]{1,0:T(8,128)(2,1)}, u32[]{:S(2)}) copy-start(bf16[512,3072]{1,0:T(8,128)(2,1)} %param.19) | copy-start | bytes 9437188
  6.6 127.4 %all-reduce.3.cloned.1.call-start = ((), (), s32[]{:S(2)}) async-start(), calls=%async_computation | async-start | bytes 786432 | tf_op jit(solution)/shard_map/psum | solution.py:49
  34.1 22.5 %copy-start.1 = (bf16[3072]{0:T(1024)(128)(2,1)S(1)}, bf16[3072]{0:T(1024)(128)(2,1)}, u32[]{:S(2)}) copy-start(bf16[3072]{0:T(1024)(128)(2,1)} %param.16) | copy-start | bytes 18436
  56.5 160.3 %all-reduce.5.cloned.1.call-start = ((), (), s32[]{:S(2)}) async-start(), calls=%async_computation.1 | async-start | bytes 786432 | tf_op jit(solution)/shard_map/psum | solution.py:49
Sparse Core Ops, SparseCore 0:
  56.6 77.2 all-reduce.2
  142.7 74.0 all-reduce.4
where the time goes:
time: 226 us
  waiting for transfers between devices  152 us (67%)
  matrix products  51 us (23%)
  between operations  13.5 us (6%)
  other arithmetic  8.91 us (4%)
    psum x2, waiting for transfers between devices, added(): lax.psum(term.astype(jnp.bfloat16), 'tp').astype(jnp.float32)  152 us
    dot_general x2, matrix products, einsum(): return jnp.einsum(form, a.astype(jnp.float32), b.astype(jnp.float32))  39.5 us
  transfers between devices with their start and end apart: 2, of which 2 were waited for; matrix products, arithmetic and copies ran while one was open for 0% of the time, Pallas kernels for 0%

commit v1 on v0

v1 whole, which is shorter than its diff:
```python
import functools

import jax
import jax.numpy as jnp
import numpy as np
from jax import lax
from jax.experimental import pallas as pl
from jax.experimental.pallas import tpu as pltpu
from jax.sharding import PartitionSpec as P

HEAD = 96
THETA = 10000
GROUP = 4
CHUNKS = 4
SLOTS = 4
MESH = pl.DeviceIdType.MESH
F32, BF16 = jnp.float32, jnp.bfloat16


def dot(a, b):
    return jnp.dot(a, b, preferred_element_type=F32)


def dot_t(a, b):
    return lax.dot_general(a, b, (((1,), (1,)), ((), ())), preferred_element_type=F32)


def normed(wide, gain):
    scale = lax.rsqrt(jnp.mean(wide * wide, -1, keepdims=True) + 1e-6)
    return (wide * scale * gain).astype(BF16)


def iota(shape, axis):
    return lax.broadcasted_iota(jnp.int32, shape, axis)


def ones_where(mask):
    return jnp.where(mask, 1.0, 0.0).astype(BF16)


def kernel(
    n, x_hbm, k_hbm, v_hbm, ga_ref, wq_hbm, wo_hbm, gm_ref, wg_hbm, wu_hbm, wd_hbm, cos_ref, sin_ref,
    y_hbm,
    x_v, wq_v, wo_v, wg_v, wu_v, wd_v, k_v, v_v, q_all, o_all, tile_m, xb_v,
    t1, r1, h_all, t2, r2, ys,
    sem_x, sem_w, sem_k, sem_v, sem_b, sem_y, s1, q1, sh, qh, s2, q2, sy, qy,
):
    batch, d = x_hbm.shape
    steps = batch // GROUP
    rows = batch // CHUNKS
    per = steps // CHUNKS
    wide = wq_hbm.shape[0]
    heads = wide // HEAD
    fold = GROUP * wide
    rh = rows // 2
    cg = n // 2
    cw = d // cg
    scale = HEAD**-0.5
    me = lax.axis_index("tp")
    mr, mc = lax.div(me, cg), lax.rem(me, cg)

    def peer_of(k):
        return lax.rem(me + k, n)

    barrier = pltpu.get_barrier_semaphore()
    for k in range(1, n):
        pl.semaphore_signal(barrier, inc=1, device_id={"tp": peer_of(k)}, device_id_type=MESH)

    cx = pltpu.make_async_copy(x_hbm, x_v, sem_x)
    cx.start()
    weights = [(wq_hbm, wq_v), (wo_hbm, wo_v), (wg_hbm, wg_v), (wu_hbm, wu_v), (wd_hbm, wd_v)]

    def weight(i):
        return pltpu.make_async_copy(*weights[i], sem_w.at[i])

    weight(0).start()

    def block_of(ref, c):
        return ref.at[pl.ds(pl.multiple_of(rows * c + rh * mr, rh), rh), pl.ds(pl.multiple_of(cw * mc, 128), cw)]

    def xblock(c):
        return pltpu.make_async_copy(block_of(x_hbm, c), xb_v.at[c], sem_b.at[c])

    def fetch(s, src, dst, sem):
        slot = lax.rem(s, SLOTS)
        return pltpu.make_async_copy(
            src.at[pl.ds(pl.multiple_of(s * fold, fold), fold)], dst.at[slot], sem.at[slot]
        )

    for s in range(SLOTS):
        fetch(s, k_hbm, k_v, sem_k).start()
        fetch(s, v_hbm, v_v, sem_v).start()
    for c in range(CHUNKS):
        xblock(c).start()

    col = iota((1, fold), 1)
    inner = col
    for i in range(1, GROUP):
        inner = inner - jnp.where(col >= i * wide, wide, 0)
    within = inner
    for i in range(1, heads):
        within = within - jnp.where(inner >= i * HEAD, HEAD, 0)
    half = HEAD // 2
    partner = jnp.where(within < half, inner + half, inner - half)
    row = iota((wide, fold), 0)
    tile_m[...] = ones_where(row == inner)
    swap_m = ones_where(row == partner)
    cx.wait()
    a = normed(x_v[...].astype(F32), ga_ref[...].astype(F32))
    weight(0).wait()
    q = dot_t(a, wq_v[...]).astype(BF16)
    turned = (dot(q, tile_m[...]) * cos_ref[...] + dot(q, swap_m) * sin_ref[...]).astype(BF16)
    spread = ones_where(iota((batch * heads, batch), 0) // heads == iota((batch * heads, batch), 1))
    place = lax.rem(iota((batch * heads, 1), 0), GROUP * heads) * HEAD
    mine = (col >= place) & (col < place + HEAD)
    q_all[...] = jnp.where(mine, dot(spread, turned), 0.0)

    pl.semaphore_wait(barrier, n - 1)

    def scatter(term, c, t, r, send, recv):
        for o in range(n):
            i, j = o // cg, o % cg
            t[c, o] = term[i * rh : (i + 1) * rh, j * cw : (j + 1) * cw].astype(BF16)
        for k in range(1, n):
            p = peer_of(k)
            pltpu.make_async_remote_copy(
                src_ref=t.at[c, p], dst_ref=r.at[c, k - 1], send_sem=send.at[c], recv_sem=recv.at[c],
                device_id={"tp": p}, device_id_type=MESH,
            ).start()

    def landed(ref, sem):
        pltpu.make_async_copy(ref, ref, sem).wait()

    def total(c, first, t, r):
        acc = t[c, me].astype(F32)
        for k in range(n - 1):
            acc = acc + r[c, k].astype(F32)
        return (first.astype(F32) + acc).astype(BF16)

    def attention(s):
        slot = lax.rem(s, SLOTS)
        at = pl.ds(pl.multiple_of(s * GROUP * heads, GROUP * heads), GROUP * heads)
        fetch(s, k_hbm, k_v, sem_k).wait()
        scores = dot(q_all[at, :].astype(BF16), k_v[slot]) * scale
        e = jnp.exp(scores - jnp.max(scores, -1, keepdims=True))
        w = (e * (1.0 / jnp.sum(e, -1, keepdims=True))).astype(BF16)
        fetch(s, v_hbm, v_v, sem_v).wait()
        o = dot_t(w, v_v[slot])
        first = iota((GROUP * heads, 1), 0) * HEAD
        o_all[at, :] = jnp.where((col >= first) & (col < first + HEAD), o, 0.0)

        @pl.when(s + SLOTS < steps)
        def _():
            fetch(s + SLOTS, k_hbm, k_v, sem_k).start()
            fetch(s + SLOTS, v_hbm, v_v, sem_v).start()

    def project(c):
        at = pl.ds(pl.multiple_of(c * rows * heads, rows * heads), rows * heads)
        folded = dot_t(o_all[at, :].astype(BF16), tile_m[...]).astype(BF16)
        gather = ones_where(iota((rows, rows * heads), 1) // heads == iota((rows, rows * heads), 0))
        seen = dot(gather, folded).astype(BF16)
        scatter(dot(seen, wo_v[...]), c, t1, r1, s1, q1)

    def states(c):
        xblock(c).wait()
        landed(r1.at[c], q1.at[c])
        h_all[c, me] = total(c, xb_v[c], t1, r1)
        for k in range(1, n):
            pltpu.make_async_remote_copy(
                src_ref=h_all.at[c, me], dst_ref=h_all.at[c, me], send_sem=sh.at[c], recv_sem=qh.at[c],
                device_id={"tp": peer_of(k)}, device_id_type=MESH,
            ).start()

    def mlp(c):
        landed(r1.at[c], qh.at[c])
        h = jnp.concatenate(
            [jnp.concatenate([h_all[c, i * cg + j].astype(F32) for j in range(cg)], 1) for i in range(2)], 0
        )
        b = normed(h, gm_ref[...].astype(F32))
        gate = dot(b, wg_v[...])
        up = dot(b, wu_v[...])
        hidden = (jax.nn.silu(gate) * up).astype(BF16)
        scatter(dot(hidden, wd_v[...]), c, t2, r2, s2, q2)

    def outputs(c):
        landed(r2.at[c], q2.at[c])
        ys[c] = total(c, h_all[c, me], t2, r2)
        pltpu.make_async_copy(ys.at[c], block_of(y_hbm, c), sem_y.at[c]).start()
        for k in range(1, n):
            pltpu.make_async_remote_copy(
                src_ref=ys.at[c], dst_ref=block_of(y_hbm, c), send_sem=sy.at[c], recv_sem=qy.at[c],
                device_id={"tp": peer_of(k)}, device_id_type=MESH,
            ).start()

    gap = 3
    stages = (project, states, mlp, outputs)
    lag = gap * (len(stages) - 1)

    def body(s, carry):
        for i in range(1, len(weights)):

            @pl.when(s == i - 1)
            def _(i=i):
                weight(i).start()

        @pl.when(s < steps)
        def _():
            attention(s)

        @pl.when(s == per - 1)
        def _():
            weight(1).wait()

        @pl.when(s == per - 1 + 2 * gap)
        def _():
            for i in range(2, len(weights)):
                weight(i).wait()

        for i, stage in enumerate(stages):
            past = s - (per - 1) - gap * i

            @pl.when((past >= 0) & (past <= per * (CHUNKS - 1)) & (lax.rem(past + per, per) == 0))
            def _(stage=stage, past=past):
                stage(lax.div(past, per))

        return carry

    lax.fori_loop(0, steps + lag, body, 0)

    for c in range(CHUNKS):
        landed(r1.at[c], s1.at[c])
        landed(r1.at[c], sh.at[c])
        landed(r2.at[c], s2.at[c])
        landed(r2.at[c], sy.at[c])
        landed(r2.at[c], qy.at[c])
        pltpu.make_async_copy(ys.at[c], block_of(y_hbm, c), sem_y.at[c]).wait()


def solution(mesh):
    n = mesh.shape["tp"]

    def step(x, k_cache, v_cache, gain_a, wq, wo, gain_m, w_gate, w_up, w_down):
        batch, cache, heads, head = k_cache.shape
        d, wide = wq.shape
        ff = w_gate.shape[1]
        fold = GROUP * wide
        rows = batch // CHUNKS
        block = (rows // 2, d // (n // 2))
        keys = jnp.transpose(k_cache, (0, 2, 3, 1)).reshape(batch * wide, cache)
        values = jnp.transpose(v_cache, (0, 2, 3, 1)).reshape(batch * wide, cache)
        half = head // 2
        angle = (cache - 1) * float(THETA) ** (-np.arange(half) / half)
        cos, sin = np.cos(angle), np.sin(angle)
        cos = np.tile(np.concatenate([cos, cos]), fold // head)[None].astype(np.float32)
        sin = np.tile(np.concatenate([-sin, sin]), fold // head)[None].astype(np.float32)
        hbm, vmem = pl.BlockSpec(memory_space=pl.ANY), pl.BlockSpec(memory_space=pltpu.VMEM)
        dma, per_chunk = pltpu.SemaphoreType.DMA, pltpu.SemaphoreType.DMA((CHUNKS,))
        return pl.pallas_call(
            functools.partial(kernel, n),
            out_shape=jax.ShapeDtypeStruct(x.shape, BF16),
            in_specs=[hbm, hbm, hbm, vmem, hbm, hbm, vmem, hbm, hbm, hbm, vmem, vmem],
            out_specs=hbm,
            scratch_shapes=[
                pltpu.VMEM((batch, d), BF16),
                pltpu.VMEM((wide, d), BF16),
                pltpu.VMEM((wide, d), BF16),
                pltpu.VMEM((d, ff), BF16),
                pltpu.VMEM((d, ff), BF16),
                pltpu.VMEM((ff, d), BF16),
                pltpu.VMEM((SLOTS, fold, cache), BF16),
                pltpu.VMEM((SLOTS, fold, cache), BF16),
                pltpu.VMEM((batch * heads, fold), F32),
                pltpu.VMEM((batch * heads, fold), F32),
                pltpu.VMEM((wide, fold), BF16),
                pltpu.VMEM((CHUNKS, *block), BF16),
                pltpu.VMEM((CHUNKS, n, *block), BF16),
                pltpu.VMEM((CHUNKS, n - 1, *block), BF16),
                pltpu.VMEM((CHUNKS, n, *block), BF16),
                pltpu.VMEM((CHUNKS, n, *block), BF16),
                pltpu.VMEM((CHUNKS, n - 1, *block), BF16),
                pltpu.VMEM((CHUNKS, *block), BF16),
                dma, dma((5,)), dma((SLOTS,)), dma((SLOTS,)), per_chunk, per_chunk,
                *[per_chunk] * 8,
            ],
            compiler_params=pltpu.CompilerParams(
                collective_id=0, has_side_effects=True, vmem_limit_bytes=62 * 2**20
            ),
        )(x, keys, values, gain_a[None], wq.T, wo, gain_m[None], w_gate, w_up, w_down, cos, sin)

    states, cache, columns, rows_of = P("dp", None), P("dp", None, "tp", None), P(None, "tp"), P("tp", None)
    return jax.shard_map(
        step,
        mesh=mesh,
        in_specs=(states, cache, cache, P(None), columns, rows_of, P(None), columns, columns, rows_of),
        out_specs=states,
        check_vma=False,
    )
```

time: 226 us -> 74.2 us (0.33)
  waiting for transfers between devices: 152 us -> 0 us
  Pallas kernels: 0 us -> 69.6 us
  matrix products: 51 us -> 0 us
  between operations: 13.5 us -> 0.01 us
  other arithmetic: 8.91 us -> 0 us
  local copies, waits for them, and re-layouts: 0.32 us -> 4.36 us
    psum x2 -> x0, waiting for transfers between devices: 152 us -> none  [added(): lax.psum(term.astype(jnp.bfloat16), 'tp').astype(jnp.float32)]
    pallas_call x0 -> x1, Pallas kernels: none -> 69.6 us  [step(): pl.pallas_call(functools.partial(kernel, n), out_shape=jax.ShapeDtypeStru...]
    dot_general x6 -> x0, matrix products: 51 us -> none  [the longest x2 39.5 us: einsum(): return jnp.einsum(form, a.astype(jnp.float32), b.astype(jnp.float32))]
    div x1 -> x0, other arithmetic: 3.44 us -> none  [seen_by(): weights = jax.nn.softmax(scores, -1).astype(jnp.bfloat16)]
    convert_element_type x4 -> x0, other arithmetic: 2.71 us -> none  [the longest x1 1.83 us: added(): (t.astype(jnp.float32) + lax.psum(term.astype(jnp.bfloat16), 'tp').astype...]
    broadcast_in_dim x0 -> x2, local copies, waits for them, and re-layouts: none -> 2.59 us  [the longest x1 1.3 us: step(): gain_a[None]]
    reduce_sum x2 -> x0, other arithmetic: 2.58 us -> none  [normed(): scale = lax.rsqrt(jnp.mean(wide * wide, -1, keepdims=True) + 1e-06)]
  transfers between devices with their start and end apart: 2 -> 0, of which waited for: 2 -> 0; matrix products, arithmetic and copies ran while one was open for 0% -> 0% of each run, Pallas kernels for 0% -> 0%
where the time goes in v1:
time: 74.2 us; the launch traced here: 74 us
  Pallas kernels  69.6 us (94%)
  local copies, waits for them, and re-layouts  4.36 us (6%)
    pallas_call x1, Pallas kernels, step(): pl.pallas_call(functools.partial(kernel, n), out_shape=jax.ShapeDtypeStru...  69.6 us
    unnamed x1, local copies, waits for them, and re-layouts  1.77 us

profile of v1, /device:TPU:96, one launch (start us, length us, event | category | flops | bytes accessed | tf_op | source)
XLA Modules:
  0.0 74.0 jit_solution(15125816221280145987)
XLA Ops:
  0.0 1.3 %broadcast_in_dim.6.ga_ref = bf16[1,3072]{1,0:T(2,128)(2,1)} reshape(bf16[3072]{0:T(1024)(128)(2,1)} %param.15) | data formatting | bytes 12288 | tf_op jit(solution)/shard_map/broadcast_in_dim | solution.py:288
  1.3 1.3 %broadcast_in_dim.7.gm_ref = bf16[1,3072]{1,0:T(2,128)(2,1)} reshape(bf16[3072]{0:T(1024)(128)(2,1)} %param.18) | data formatting | bytes 12288 | tf_op jit(solution)/shard_map/broadcast_in_dim | solution.py:288
  2.6 69.6 %shard_map.118 = bf16[64,3072]{1,0:T(8,128)(2,1)} custom-call(bf16[64,3072]{1,0:T(8,128)(2,1)} %x_hbm.1, bf16[12288,2048]{1,0:T(8,128)(2,1)} %bitcast.7, bf16[12288,2048]{1,0:T(8,128)(2,1)} %bitcast.8, bf16[1,3072]{1,0:T(2,128)(2,1)} %broadcast_in_dim.6.ga_ref, bf16[192,3072]{1,0:T(8,128)(2,1)} %bitcast.9, bf16[192,3072]{1,0:T(8,128)(2,1)} %wo_hbm.1, ...), custom_call_target="tpu_custom_call" | custom-call | tf_op jit(solution)/shard_map/pallas_call | solution.py:258
  72.2 1.8 %copy.14 = bf16[64,3072]{1,0:T(8,128)(2,1)} copy(bf16[64,3072]{1,0:T(8,128)(2,1)} %shard_map.118) | data formatting | bytes 786432

commit v2 on v1

v2 whole, which is shorter than its diff:
```python
import functools

import jax
import jax.numpy as jnp
import numpy as np
from jax import lax
from jax.experimental import pallas as pl
from jax.experimental.pallas import tpu as pltpu
from jax.sharding import PartitionSpec as P

HEAD = 96
THETA = 10000
GROUP = 4
CHUNKS = 4
SLOTS = 4
MESH = pl.DeviceIdType.MESH
F32, BF16 = jnp.float32, jnp.bfloat16


def dot(a, b):
    return jnp.dot(a, b, preferred_element_type=F32)


def dot_t(a, b):
    return lax.dot_general(a, b, (((1,), (1,)), ((), ())), preferred_element_type=F32)


def normed(wide, gain):
    scale = lax.rsqrt(jnp.mean(wide * wide, -1, keepdims=True) + 1e-6)
    return (wide * scale * gain).astype(BF16)


def iota(shape, axis):
    return lax.broadcasted_iota(jnp.int32, shape, axis)


def ones_where(mask):
    return jnp.where(mask, 1.0, 0.0).astype(BF16)


def kernel(
    n, x_hbm, k_hbm, v_hbm, ga_hbm, wq_hbm, wo_hbm, gm_hbm, wg_hbm, wu_hbm, wd_hbm, cs_hbm,
    y_hbm,
    x_v, ga_v, gm_v, cs_v, wq_v, wo_v, wg_v, wu_v, wd_v, k_v, v_v, q_all, seen_all, xb_v,
    t1, r1, h_all, te, re, tl, rl, ys,
    sem_i, sem_w, sem_k, sem_v, sem_b, sem_y, s1, q1, sh, qh, s2, q2, sy, qy,
):
    batch, d = x_hbm.shape
    steps = batch // GROUP
    rows = batch // CHUNKS
    per = steps // CHUNKS
    early = CHUNKS - 1
    wide = wq_hbm.shape[0]
    heads = wide // HEAD
    fold = GROUP * wide
    rh = rows // 2
    cg = n // 2
    cw = d // cg
    scale = HEAD**-0.5
    me = lax.axis_index("tp")
    mr, mc = lax.div(me, cg), lax.rem(me, cg)

    def peer_of(k):
        return lax.rem(me + k, n)

    first = [
        pltpu.make_async_copy(a, b, sem_i.at[i])
        for i, (a, b) in enumerate([(x_hbm, x_v), (ga_hbm, ga_v), (wq_hbm, wq_v), (cs_hbm, cs_v), (gm_hbm, gm_v)])
    ]
    for copy in first:
        copy.start()
    weights = [(wo_hbm, wo_v), (wg_hbm, wg_v), (wu_hbm, wu_v), (wd_hbm, wd_v)]

    def weight(i):
        return pltpu.make_async_copy(*weights[i], sem_w.at[i])

    def block_of(ref, c):
        return ref.at[pl.ds(pl.multiple_of(rows * c + rh * mr, rh), rh), pl.ds(pl.multiple_of(cw * mc, 128), cw)]

    def xblock(c):
        return pltpu.make_async_copy(block_of(x_hbm, c), xb_v.at[c], sem_b.at[c])

    def fetch(s, src, dst, sem):
        slot = lax.rem(s, SLOTS)
        return pltpu.make_async_copy(
            src.at[pl.ds(pl.multiple_of(s * fold, fold), fold)], dst.at[slot], sem.at[slot]
        )

    for s in range(SLOTS):
        fetch(s, k_hbm, k_v, sem_k).start(priority=1)
        fetch(s, v_hbm, v_v, sem_v).start(priority=1)
    for c in range(CHUNKS):
        xblock(c).start(priority=1)
    weight(0).start(priority=1)

    barrier = pltpu.get_barrier_semaphore()
    for k in range(1, n):
        pl.semaphore_signal(barrier, inc=1, device_id={"tp": peer_of(k)}, device_id_type=MESH)

    col = iota((1, fold), 1)
    inner = col
    for i in range(1, GROUP):
        inner = inner - jnp.where(col >= i * wide, wide, 0)
    within = inner
    for i in range(1, heads):
        within = within - jnp.where(inner >= i * HEAD, HEAD, 0)
    half = HEAD // 2
    partner = jnp.where(within < half, inner + half, inner - half)
    row = iota((wide, fold), 0)
    tile_m, swap_m = ones_where(row == inner), ones_where(row == partner)

    def place(r):
        return lax.rem(r, GROUP) * wide + lax.div(r, GROUP) * HEAD

    def gain_of(ref):
        g = ref[...].astype(F32)
        return jnp.concatenate([g[i : i + 1] for i in range(g.shape[0])], 1)

    first[0].wait()
    first[1].wait()
    a = normed(x_v[...].astype(F32), gain_of(ga_v))
    first[2].wait()
    q = dot_t(a, wq_v[...]).astype(BF16)
    first[3].wait()
    turned = (dot(q, tile_m) * cs_v[0:1] + dot(q, swap_m) * cs_v[1:2]).astype(BF16)
    many = GROUP * heads
    r = iota((batch * heads, batch), 0)
    spread = ones_where(lax.div(r, many) * GROUP + lax.rem(r, GROUP) == iota((batch * heads, batch), 1))
    at = place(lax.rem(iota((batch * heads, 1), 0), many))
    q_all[...] = jnp.where((col >= at) & (col < at + HEAD), dot(spread, turned), 0.0)

    pl.semaphore_wait(barrier, n - 1)

    def send(src, dst, sems, k):
        pltpu.make_async_remote_copy(
            src_ref=src, dst_ref=dst, send_sem=sems[0], recv_sem=sems[1],
            device_id={"tp": peer_of(k)}, device_id_type=MESH,
        ).start()

    def landed(ref, sem):
        pltpu.make_async_copy(ref, ref, sem).wait()

    def cut(term, t):
        for o in range(n):
            i, j = o // cg, o % cg
            for c in range(term.shape[0] // rows):
                t[o, c * rh : (c + 1) * rh] = term[
                    c * rows + i * rh : c * rows + (i + 1) * rh, j * cw : (j + 1) * cw
                ].astype(BF16)

    def scatter(t, r, sems):
        for k in range(1, n):
            send(t.at[peer_of(k)], r.at[k - 1], sems, k)

    def total(first, t, r):
        acc = t[me].astype(F32)
        for k in range(n - 1):
            acc = acc + r[k].astype(F32)
        return (first + acc).astype(BF16)

    def attention(s):
        slot = lax.rem(s, SLOTS)
        at = pl.ds(pl.multiple_of(s * many, many), many)
        fetch(s, k_hbm, k_v, sem_k).wait()
        scores = dot(q_all[at, :].astype(BF16), k_v[slot]) * scale
        e = jnp.exp(scores - jnp.max(scores, -1, keepdims=True))
        w = (e * (1.0 / jnp.sum(e, -1, keepdims=True))).astype(BF16)
        fetch(s, v_hbm, v_v, sem_v).wait()
        o = dot_t(w, v_v[slot])
        start = place(iota((many, 1), 0))
        o = jnp.where((col >= start) & (col < start + HEAD), o, 0.0)
        o = o[:, : fold // 2] + o[:, fold // 2 :]
        o = o + pltpu.roll(o, fold // 4, axis=1)
        seen_all[s] = o[:GROUP, :wide] + o[GROUP:, :wide]

        @pl.when(s + SLOTS < steps)
        def _():
            fetch(s + SLOTS, k_hbm, k_v, sem_k).start(priority=1)
            fetch(s + SLOTS, v_hbm, v_v, sem_v).start(priority=1)

    def project(c):
        seen = jnp.concatenate([seen_all[c * per + i] for i in range(per)], 0).astype(BF16)
        cut(dot(seen, wo_v[...]), t1.at[c])
        scatter(t1.at[c], r1.at[c], (s1.at[c], q1.at[c]))

    def states(c):
        xblock(c).wait()
        landed(r1.at[c], q1.at[c])
        h_all[c, me] = total(xb_v[c].astype(F32), t1.at[c], r1.at[c])
        for k in range(1, n):
            send(h_all.at[c, me], h_all.at[c, me], (sh.at[c], qh.at[c]), k)

    def mlp(chunks, t):
        for c in chunks:
            landed(r1.at[c], qh.at[c])
        h = jnp.concatenate(
            [
                jnp.concatenate([h_all[c, i * cg + j].astype(F32) for j in range(cg)], 1)
                for c in chunks
                for i in range(2)
            ],
            0,
        )
        b = normed(h, gain_of(gm_v))
        gate = dot(b, wg_v[...])
        up = dot(b, wu_v[...])
        hidden = (jax.nn.silu(gate) * up).astype(BF16)
        cut(dot(hidden, wd_v[...]), t)

    def outputs(chunks, t, r, sem):
        landed(r, sem)
        h = jnp.concatenate([h_all[c, me].astype(F32) for c in chunks], 0)
        y = total(h, t, r)
        for i, c in enumerate(chunks):
            ys[c] = y[i * rh : (i + 1) * rh]
        for c in chunks:
            pltpu.make_async_copy(ys.at[c], block_of(y_hbm, c), sem_y.at[c]).start()
            for k in range(1, n):
                send(ys.at[c], block_of(y_hbm, c), (sy.at[c], qy.at[c]), k)

    def body(s, carry):
        attention(s)

        @pl.when(s == steps - SLOTS - 1)
        def _():
            for i in range(1, len(weights)):
                weight(i).start(priority=1)

        @pl.when(s == per - 1)
        def _():
            weight(0).wait()

        @pl.when(lax.rem(s, per) == per - 1)
        def _():
            project(lax.div(s, per))

        @pl.when((s >= per) & (lax.rem(s, per) == per - 2))
        def _():
            states(lax.div(s, per) - 1)

        return carry

    lax.fori_loop(0, steps, body, 0)

    first[4].wait()
    for i in range(1, len(weights)):
        weight(i).wait()
    head, last = list(range(early)), [early]
    mlp(head, te)
    states(early)
    scatter(te, re, (s2.at[0], q2.at[0]))
    mlp(last, tl)
    scatter(tl, rl, (s2.at[1], q2.at[1]))
    outputs(head, te, re, q2.at[0])
    outputs(last, tl, rl, q2.at[1])

    landed(re, s2.at[0])
    landed(rl, s2.at[1])
    for c in range(CHUNKS):
        landed(r1.at[c], s1.at[c])
        landed(r1.at[c], sh.at[c])
        landed(r1.at[c], sy.at[c])
        landed(r1.at[c], qy.at[c])
        pltpu.make_async_copy(ys.at[c], block_of(y_hbm, c), sem_y.at[c]).wait()


def solution(mesh):
    n = mesh.shape["tp"]

    def step(x, k_cache, v_cache, gain_a, wq, wo, gain_m, w_gate, w_up, w_down):
        batch, cache, heads, head = k_cache.shape
        d, wide = wq.shape
        ff = w_gate.shape[1]
        fold = GROUP * wide
        rows = batch // CHUNKS
        block = (rows // 2, d // (n // 2))
        keys = jnp.transpose(k_cache, (0, 2, 3, 1)).reshape(batch * wide, cache)
        values = jnp.transpose(v_cache, (0, 2, 3, 1)).reshape(batch * wide, cache)
        half = head // 2
        angle = (cache - 1) * float(THETA) ** (-np.arange(half) / half)
        cos, sin = np.cos(angle), np.sin(angle)
        turn = np.stack([np.tile([*cos, *cos], fold // head), np.tile([*-sin, *sin], fold // head)]).astype(np.float32)
        hbm = pl.BlockSpec(memory_space=pl.ANY)
        gains = (d // 128, 128)
        dma, per_chunk = pltpu.SemaphoreType.DMA, pltpu.SemaphoreType.DMA((CHUNKS,))
        return pl.pallas_call(
            functools.partial(kernel, n),
            out_shape=jax.ShapeDtypeStruct(x.shape, BF16),
            in_specs=[hbm] * 11,
            out_specs=hbm,
            scratch_shapes=[
                pltpu.VMEM((batch, d), BF16),
                pltpu.VMEM(gains, BF16),
                pltpu.VMEM(gains, BF16),
                pltpu.VMEM((2, fold), F32),
                pltpu.VMEM((wide, d), BF16),
                pltpu.VMEM((wide, d), BF16),
                pltpu.VMEM((d, ff), BF16),
                pltpu.VMEM((d, ff), BF16),
                pltpu.VMEM((ff, d), BF16),
                pltpu.VMEM((SLOTS, fold, cache), BF16),
                pltpu.VMEM((SLOTS, fold, cache), BF16),
                pltpu.VMEM((batch * heads, fold), F32),
                pltpu.VMEM((batch // GROUP, GROUP, wide), F32),
                pltpu.VMEM((CHUNKS, *block), BF16),
                pltpu.VMEM((CHUNKS, n, *block), BF16),
                pltpu.VMEM((CHUNKS, n - 1, *block), BF16),
                pltpu.VMEM((CHUNKS, n, *block), BF16),
                pltpu.VMEM((n, (CHUNKS - 1) * block[0], block[1]), BF16),
                pltpu.VMEM((n - 1, (CHUNKS - 1) * block[0], block[1]), BF16),
                pltpu.VMEM((n, *block), BF16),
                pltpu.VMEM((n - 1, *block), BF16),
                pltpu.VMEM((CHUNKS, *block), BF16),
                dma((5,)), dma((4,)), dma((SLOTS,)), dma((SLOTS,)), per_chunk, per_chunk,
                *[per_chunk] * 4, dma((2,)), dma((2,)), per_chunk, per_chunk,
            ],
            compiler_params=pltpu.CompilerParams(
                collective_id=0, has_side_effects=True, vmem_limit_bytes=62 * 2**20
            ),
        )(x, keys, values, gain_a.reshape(gains), wq.T, wo, gain_m.reshape(gains), w_gate, w_up, w_down, turn)

    states, cache, columns, rows_of = P("dp", None), P("dp", None, "tp", None), P(None, "tp"), P("tp", None)
    return jax.shard_map(
        step,
        mesh=mesh,
        in_specs=(states, cache, cache, P(None), columns, rows_of, P(None), columns, columns, rows_of),
        out_specs=states,
        check_vma=False,
    )
```

time: 74.2 us -> 62.2 us (0.84)
  Pallas kernels: 69.6 us -> 60.3 us
  local copies, waits for them, and re-layouts: 4.36 us -> 1.77 us
    pallas_call x1, Pallas kernels: 69.6 us -> 60.3 us  [step(): pl.pallas_call(functools.partial(kernel, n), out_shape=jax.ShapeDtypeStru...]
    broadcast_in_dim x2 -> x0, local copies, waits for them, and re-layouts: 2.59 us -> none  [the longest x1 1.3 us: step(): gain_a[None]]
where the time goes in v2:
time: 62.2 us; the launch traced here: 62.1 us
  Pallas kernels  60.3 us (97%)
  local copies, waits for them, and re-layouts  1.77 us (3%)
    pallas_call x1, Pallas kernels, step(): pl.pallas_call(functools.partial(kernel, n), out_shape=jax.ShapeDtypeStru...  60.3 us
    unnamed x1, local copies, waits for them, and re-layouts  1.77 us

profile of v2, /device:TPU:96, one launch (start us, length us, event | category | flops | bytes accessed | tf_op | source)
XLA Modules:
  0.0 62.1 jit_solution(7108822073775673972)
XLA Ops:
  0.0 60.3 %shard_map.109 = bf16[64,3072]{1,0:T(8,128)(2,1)} custom-call(bf16[64,3072]{1,0:T(8,128)(2,1)} %x_hbm.1, bf16[12288,2048]{1,0:T(8,128)(2,1)} %bitcast.9, bf16[12288,2048]{1,0:T(8,128)(2,1)} %bitcast.10, bf16[24,128]{1,0:T(8,128)(2,1)} %bitcast.12, bf16[192,3072]{1,0:T(8,128)(2,1)} %bitcast.11, bf16[192,3072]{1,0:T(8,128)(2,1)} %wo_hbm.1, ...), custom_call_target="tpu_custom_call" | custom-call | tf_op jit(solution)/shard_map/pallas_call | solution.py:286
  60.3 1.8 %copy.13 = bf16[64,3072]{1,0:T(8,128)(2,1)} copy(bf16[64,3072]{1,0:T(8,128)(2,1)} %shard_map.109) | data formatting | bytes 786432

commit v3 on v2

v3 whole, which is shorter than its diff:
```python
import functools
import math

import jax
import jax.numpy as jnp
import numpy as np
from jax import lax
from jax.experimental import pallas as pl
from jax.experimental.pallas import tpu as pltpu
from jax.sharding import PartitionSpec as P

HEAD = 96
THETA = 10000
GROUP = 4
CHUNKS = 4
LEAD = 1
SLOTS = 4
MESH = pl.DeviceIdType.MESH
F32, BF16 = jnp.float32, jnp.bfloat16


def dot(a, b):
    return jnp.dot(a, b, preferred_element_type=F32)


def dot_t(a, b):
    return lax.dot_general(a, b, (((1,), (1,)), ((), ())), preferred_element_type=F32)


def normed(wide, gain):
    scale = lax.rsqrt(jnp.mean(wide * wide, -1, keepdims=True) + 1e-6)
    return (wide * scale * gain).astype(BF16)


def iota(shape, axis):
    return lax.broadcasted_iota(jnp.int32, shape, axis)


def ones_where(mask):
    return jnp.where(mask, 1.0, 0.0).astype(BF16)


def kernel(
    n, x_hbm, k_hbm, v_hbm, ga_hbm, wq_hbm, wo_hbm, gm_hbm, wg_hbm, wu_hbm, wd_hbm, cs_hbm,
    y_hbm,
    x_v, ga_v, gm_v, cs_v, wq_v, wo_v, wg_v, wu_v, wd_v, k_v, v_v, q_all, scores, seen_all, xb_v,
    t1, r1, h_all, t2, r2, ys,
    sem_i, sem_w, sem_k, sem_v, sem_b, sem_y, s1, q1, sh, qh, s2, q2, sy, qy,
):
    batch, d = x_hbm.shape
    steps = batch // GROUP
    rows = batch // CHUNKS
    per = steps // CHUNKS
    early = CHUNKS - 1
    wide = wq_hbm.shape[0]
    heads = wide // HEAD
    fold = GROUP * wide
    rh = rows // 2
    cg = n // 2
    cw = d // cg
    scale = HEAD**-0.5
    me = lax.axis_index("tp")
    mr, mc = lax.div(me, cg), lax.rem(me, cg)

    side = math.isqrt(n)
    away = [min(i, side - i) for i in range(side)]
    moves = sorted(
        ((i, j) for i in range(side) for j in range(side) if i + j), key=lambda m: (-away[m[0]] - away[m[1]], m)
    )
    peers = [
        lax.rem(lax.div(me, side) + i, side) * side + lax.rem(lax.rem(me, side) + j, side) for i, j in moves
    ]

    first = [
        pltpu.make_async_copy(a, b, sem_i.at[i])
        for i, (a, b) in enumerate([(x_hbm, x_v), (ga_hbm, ga_v), (wq_hbm, wq_v), (cs_hbm, cs_v), (gm_hbm, gm_v)])
    ]
    for copy in first:
        copy.start()
    weights = [(wo_hbm, wo_v), (wg_hbm, wg_v), (wu_hbm, wu_v), (wd_hbm, wd_v)]

    def weight(i):
        return pltpu.make_async_copy(*weights[i], sem_w.at[i])

    def block_of(ref, c):
        return ref.at[2 * c + mr, :, pl.ds(pl.multiple_of(cw * mc, 128), cw)]

    x_rows = x_hbm.reshape(batch // rh, rh, d)

    def xblock(c):
        return pltpu.make_async_copy(block_of(x_rows, c), xb_v.at[c], sem_b.at[c])

    def fetch(s, src, dst, sem):
        slot = lax.rem(s, SLOTS)
        return pltpu.make_async_copy(
            src.at[pl.ds(pl.multiple_of(s * fold, fold), fold)], dst.at[slot], sem.at[slot]
        )

    for s in range(SLOTS + LEAD):
        if s < SLOTS:
            fetch(s, k_hbm, k_v, sem_k).start(priority=1)
        if s >= LEAD:
            fetch(s - LEAD, v_hbm, v_v, sem_v).start(priority=1)
    for c in range(CHUNKS):
        xblock(c).start(priority=1)
    weight(0).start(priority=1)

    barrier = pltpu.get_barrier_semaphore()
    for p in peers:
        pl.semaphore_signal(barrier, inc=1, device_id={"tp": p}, device_id_type=MESH)

    col = iota((1, fold), 1)
    inner = col
    for i in range(1, GROUP):
        inner = inner - jnp.where(col >= i * wide, wide, 0)
    within = inner
    for i in range(1, heads):
        within = within - jnp.where(inner >= i * HEAD, HEAD, 0)
    half = HEAD // 2
    partner = jnp.where(within < half, inner + half, inner - half)
    row = iota((wide, fold), 0)
    tile_m, swap_m = ones_where(row == inner), ones_where(row == partner)

    def place(r):
        return lax.rem(r, GROUP) * wide + lax.div(r, GROUP) * HEAD

    def gain_of(ref):
        g = ref[...].astype(F32)
        return jnp.concatenate([g[i : i + 1] for i in range(g.shape[0])], 1)

    first[0].wait()
    first[1].wait()
    a = normed(x_v[...].astype(F32), gain_of(ga_v))
    first[2].wait()
    q = dot_t(a, wq_v[...]).astype(BF16)
    first[3].wait()
    turned = (dot(q, tile_m) * cs_v[0:1] + dot(q, swap_m) * cs_v[1:2]).astype(BF16)
    many = GROUP * heads
    r = iota((batch * heads, batch), 0)
    spread = ones_where(lax.div(r, many) * GROUP + lax.rem(r, GROUP) == iota((batch * heads, batch), 1))
    at = place(lax.rem(iota((batch * heads, 1), 0), many))
    q_all[...] = jnp.where((col >= at) & (col < at + HEAD), dot(spread, turned), 0.0)

    def send(src, dst, sems, peer):
        pltpu.make_async_remote_copy(
            src_ref=src, dst_ref=dst, send_sem=sems[0], recv_sem=sems[1],
            device_id={"tp": peer}, device_id_type=MESH,
        ).start()

    def landed(ref, sem):
        pltpu.make_async_copy(ref, ref, sem).wait()

    def cut(term, chunks, t):
        for a, c in enumerate(chunks):
            for o in range(n):
                i = a * rows + o // cg * rh
                t[c, o] = term[i : i + rh, o % cg * cw : (o % cg + 1) * cw].astype(BF16)

    def scatter(t, r, sems):
        for k, p in enumerate(peers):
            send(t.at[p], r.at[k], sems, p)

    def total(first, t, r):
        acc = t[me].astype(F32)
        for k in range(n - 1):
            acc = acc + r[k].astype(F32)
        return (first + acc).astype(BF16)

    def step_rows(s):
        return pl.ds(pl.multiple_of(s * many, many), many)

    def qk(s):
        scores[lax.rem(s, LEAD + 1)] = dot(q_all[step_rows(s), :].astype(BF16), k_v[lax.rem(s, SLOTS)]) * scale

    def weights_of(s):
        t = scores[lax.rem(s, LEAD + 1)]
        e = jnp.exp(t - jnp.max(t, -1, keepdims=True))
        return (e * (1.0 / jnp.sum(e, -1, keepdims=True))).astype(BF16)

    def pv(s, w):
        o = dot_t(w, v_v[lax.rem(s, SLOTS)])
        start = place(iota((many, 1), 0))
        o = jnp.where((col >= start) & (col < start + HEAD), o, 0.0)
        o = o[:, : fold // 2] + o[:, fold // 2 :]
        o = o + pltpu.roll(o, fold // 4, axis=1)
        seen_all[s] = o[:GROUP, :wide] + o[GROUP:, :wide]

    def keys_in(s):
        return fetch(s, k_hbm, k_v, sem_k)

    def values_in(s):
        return fetch(s, v_hbm, v_v, sem_v)

    def attention(s):
        keys_in(s + LEAD).wait()
        values_in(s).wait()
        w = weights_of(s)
        qk(s + LEAD)
        pv(s, w)

        @pl.when(s + LEAD + SLOTS < steps)
        def _():
            keys_in(s + LEAD + SLOTS).start(priority=1)

        @pl.when(s + SLOTS < steps)
        def _():
            values_in(s + SLOTS).start(priority=1)

    def project(c):
        seen = jnp.concatenate([seen_all[c * per + i] for i in range(per)], 0).astype(BF16)
        cut(dot(seen, wo_v[...]), [c], t1)
        scatter(t1.at[c], r1.at[c], (s1.at[c], q1.at[c]))

    def states(c):
        xblock(c).wait()
        landed(r1.at[c], q1.at[c])
        h_all[c, me] = total(xb_v[c].astype(F32), t1.at[c], r1.at[c])
        for p in peers:
            send(h_all.at[c, me], h_all.at[c, me], (sh.at[c], qh.at[c]), p)

    def mlp(chunks):
        for c in chunks:
            landed(r1.at[c], qh.at[c])
        h = jnp.concatenate(
            [
                jnp.concatenate([h_all[c, i * cg + j].astype(F32) for j in range(cg)], 1)
                for c in chunks
                for i in range(2)
            ],
            0,
        )
        b = normed(h, gain_of(gm_v))
        gate = dot(b, wg_v[...])
        up = dot(b, wu_v[...])
        hidden = (jax.nn.silu(gate) * up).astype(BF16)
        cut(dot(hidden, wd_v[...]), chunks, t2)

    def scatter2(c):
        scatter(t2.at[c], r2.at[c], (s2.at[c], q2.at[c]))

    def outputs(c):
        landed(r2.at[c], q2.at[c])
        ys[c] = total(h_all[c, me].astype(F32), t2.at[c], r2.at[c])
        pltpu.make_async_copy(ys.at[c], block_of(y_hbm, c), sem_y.at[c]).start()
        for p in peers:
            send(ys.at[c], block_of(y_hbm, c), (sy.at[c], qy.at[c]), p)

    def between(s):
        @pl.when(s == steps - SLOTS - 1)
        def _():
            for i in range(1, len(weights)):
                weight(i).start(priority=1)

        @pl.when(s == per - 1)
        def _():
            weight(0).wait()
            pl.semaphore_wait(barrier, n - 1)

        @pl.when(lax.rem(s, per) == per - 1)
        def _():
            project(lax.div(s, per))

        @pl.when((s >= per) & (s < steps - per) & (lax.rem(s, per) == per - 2))
        def _():
            states(lax.div(s, per) - 1)

    def body(s, carry):
        attention(s)
        between(s)
        return carry

    for s in range(LEAD):
        keys_in(s).wait()
        qk(s)
        keys_in(s + SLOTS).start(priority=1)
    lax.fori_loop(0, steps - LEAD, body, 0)
    for s in range(steps - LEAD, steps):
        w = weights_of(s)
        values_in(s).wait()
        pv(s, w)
    project(early)
    states(early - 1)
    first[4].wait()
    for i in range(1, len(weights)):
        weight(i).wait()
    mlp(range(early - 1))
    for c in range(early - 1):
        scatter2(c)
    states(early)
    mlp([early - 1])
    scatter2(early - 1)
    outputs(0)
    mlp([early])
    scatter2(early)
    for c in range(1, CHUNKS):
        outputs(c)

    for c in range(CHUNKS):
        landed(r1.at[c], s1.at[c])
        landed(r1.at[c], sh.at[c])
        landed(r1.at[c], s2.at[c])
        landed(r1.at[c], sy.at[c])
        landed(r1.at[c], qy.at[c])
        pltpu.make_async_copy(ys.at[c], block_of(y_hbm, c), sem_y.at[c]).wait()


def solution(mesh):
    n = mesh.shape["tp"]

    def step(x, k_cache, v_cache, gain_a, wq, wo, gain_m, w_gate, w_up, w_down):
        batch, cache, heads, head = k_cache.shape
        d, wide = wq.shape
        ff = w_gate.shape[1]
        fold = GROUP * wide
        rows = batch // CHUNKS
        block = (rows // 2, d // (n // 2))
        keys = jnp.transpose(k_cache, (0, 2, 3, 1)).reshape(batch * wide, cache)
        values = jnp.transpose(v_cache, (0, 2, 3, 1)).reshape(batch * wide, cache)
        half = head // 2
        angle = (cache - 1) * float(THETA) ** (-np.arange(half) / half)
        cos, sin = np.cos(angle), np.sin(angle)
        turn = np.stack([np.tile([*cos, *cos], fold // head), np.tile([*-sin, *sin], fold // head)]).astype(np.float32)
        hbm = pl.BlockSpec(memory_space=pltpu.HBM)
        gains = (d // 128, 128)
        dma, per_chunk = pltpu.SemaphoreType.DMA, pltpu.SemaphoreType.DMA((CHUNKS,))
        return pl.pallas_call(
            functools.partial(kernel, n),
            out_shape=pltpu.VMEM((batch // block[0], block[0], d), BF16),
            in_specs=[hbm] * 11,
            out_specs=pl.BlockSpec(memory_space=pltpu.VMEM),
            scratch_shapes=[
                pltpu.VMEM((batch, d), BF16),
                pltpu.VMEM(gains, BF16),
                pltpu.VMEM(gains, BF16),
                pltpu.VMEM((2, fold), F32),
                pltpu.VMEM((wide, d), BF16),
                pltpu.VMEM((wide, d), BF16),
                pltpu.VMEM((d, ff), BF16),
                pltpu.VMEM((d, ff), BF16),
                pltpu.VMEM((ff, d), BF16),
                pltpu.VMEM((SLOTS, fold, cache), BF16),
                pltpu.VMEM((SLOTS, fold, cache), BF16),
                pltpu.VMEM((batch * heads, fold), F32),
                pltpu.VMEM((LEAD + 1, GROUP * heads, cache), F32),
                pltpu.VMEM((batch // GROUP, GROUP, wide), F32),
                pltpu.VMEM((CHUNKS, *block), BF16),
                pltpu.VMEM((CHUNKS, n, *block), BF16),
                pltpu.VMEM((CHUNKS, n - 1, *block), BF16),
                pltpu.VMEM((CHUNKS, n, *block), BF16),
                pltpu.VMEM((CHUNKS, n, *block), BF16),
                pltpu.VMEM((CHUNKS, n - 1, *block), BF16),
                pltpu.VMEM((CHUNKS, *block), BF16),
                dma((5,)), dma((4,)), dma((SLOTS,)), dma((SLOTS,)), per_chunk, per_chunk,
                *[per_chunk] * 8,
            ],
            compiler_params=pltpu.CompilerParams(
                collective_id=0, has_side_effects=True, vmem_limit_bytes=60 * 2**20
            ),
        )(x, keys, values, gain_a.reshape(gains), wq.T, wo, gain_m.reshape(gains), w_gate, w_up, w_down, turn).reshape(x.shape)

    states, cache, columns, rows_of = P("dp", None), P("dp", None, "tp", None), P(None, "tp"), P("tp", None)
    return jax.shard_map(
        step,
        mesh=mesh,
        in_specs=(states, cache, cache, P(None), columns, rows_of, P(None), columns, columns, rows_of),
        out_specs=states,
        check_vma=False,
    )
```

time: 62.2 us -> 59.6 us (0.958)
  Pallas kernels: 60.3 us -> 58.8 us
  local copies, waits for them, and re-layouts: 1.77 us -> 0.75 us
    pallas_call x1, Pallas kernels: 60.3 us -> 58.8 us  [step(): pl.pallas_call(functools.partial(kernel, n), out_shape=pltpu.VMEM((batch...]
    unnamed x1, local copies, waits for them, and re-layouts: 1.77 us -> 0.75 us
where the time goes in v3:
time: 59.6 us; the launch traced here: 59.5 us
  Pallas kernels  58.8 us (99%)
  local copies, waits for them, and re-layouts  0.75 us (1%)
    pallas_call x1, Pallas kernels, step(): pl.pallas_call(functools.partial(kernel, n), out_shape=pltpu.VMEM((batch...  58.8 us

profile of v3, /device:TPU:96, one launch (start us, length us, event | category | flops | bytes accessed | tf_op | source)
XLA Modules:
  0.0 59.5 jit_solution(298724282054417032)
XLA Ops:
  0.0 58.8 %shard_map.109 = bf16[8,8,3072]{2,1,0:T(8,128)(2,1)S(1)} custom-call(bf16[64,3072]{1,0:T(8,128)(2,1)} %x_hbm.1, bf16[12288,2048]{1,0:T(8,128)(2,1)} %bitcast.11, bf16[12288,2048]{1,0:T(8,128)(2,1)} %bitcast.12, bf16[24,128]{1,0:T(8,128)(2,1)} %bitcast.14, bf16[192,3072]{1,0:T(8,128)(2,1)} %bitcast.13, bf16[192,3072]{1,0:T(8,128)(2,1)} %wo_hbm.1, ...), custom_call_target="tpu_custom_call" | custom-call | tf_op jit(solution)/shard_map/pallas_call | solution.py:326
  58.8 0.7 %copy.13 = bf16[64,3072]{1,0:T(8,128)(2,1)} copy(bf16[64,3072]{1,0:T(8,128)(2,1)S(1)} %bitcast.10) | data formatting | bytes 786432

commit v4 on v3

--- a/solution.py
+++ b/solution.py
@@ -12,7 +12,7 @@
 HEAD = 96
 THETA = 10000
 GROUP = 4
-CHUNKS = 4
+QUARTER = 4
 LEAD = 1
 SLOTS = 4
 MESH = pl.DeviceIdType.MESH
@@ -44,14 +44,16 @@
     n, x_hbm, k_hbm, v_hbm, ga_hbm, wq_hbm, wo_hbm, gm_hbm, wg_hbm, wu_hbm, wd_hbm, cs_hbm,
     y_hbm,
     x_v, ga_v, gm_v, cs_v, wq_v, wo_v, wg_v, wu_v, wd_v, k_v, v_v, q_all, scores, seen_all, xb_v,
-    t1, r1, h_all, t2, r2, ys,
+    t1, r1, h_all, t2, r2, ys, a1, b1, a2, b2, h_part,
     sem_i, sem_w, sem_k, sem_v, sem_b, sem_y, s1, q1, sh, qh, s2, q2, sy, qy,
+    sa1, qa1, sb1, qb1, sa2, qa2, sb2, qb2,
 ):
     batch, d = x_hbm.shape
     steps = batch // GROUP
-    rows = batch // CHUNKS
-    per = steps // CHUNKS
-    early = CHUNKS - 1
+    rows = batch // QUARTER
+    per = steps // QUARTER
+    chunks = QUARTER - 1
+    small = rows // 2
     wide = wq_hbm.shape[0]
     heads = wide // HEAD
     fold = GROUP * wide
@@ -63,6 +65,7 @@
     mr, mc = lax.div(me, cg), lax.rem(me, cg)
 
     side = math.isqrt(n)
+    my = (lax.div(me, side), lax.rem(me, side))
     away = [min(i, side - i) for i in range(side)]
     moves = sorted(
         ((i, j) for i in range(side) for j in range(side) if i + j), key=lambda m: (-away[m[0]] - away[m[1]], m)
@@ -101,7 +104,7 @@
             fetch(s, k_hbm, k_v, sem_k).start(priority=1)
         if s >= LEAD:
             fetch(s - LEAD, v_hbm, v_v, sem_v).start(priority=1)
-    for c in range(CHUNKS):
+    for c in range(chunks):
         xblock(c).start(priority=1)
     weight(0).start(priority=1)
 
@@ -150,8 +153,8 @@
     def landed(ref, sem):
         pltpu.make_async_copy(ref, ref, sem).wait()
 
-    def cut(term, chunks, t):
-        for a, c in enumerate(chunks):
+    def cut(term, cs, t):
+        for a, c in enumerate(cs):
             for o in range(n):
                 i = a * rows + o // cg * rh
                 t[c, o] = term[i : i + rh, o % cg * cw : (o % cg + 1) * cw].astype(BF16)
@@ -218,22 +221,54 @@
         for p in peers:
             send(h_all.at[c, me], h_all.at[c, me], (sh.at[c], qh.at[c]), p)
 
-    def mlp(chunks):
-        for c in chunks:
-            landed(r1.at[c], qh.at[c])
-        h = jnp.concatenate(
-            [
-                jnp.concatenate([h_all[c, i * cg + j].astype(F32) for j in range(cg)], 1)
-                for c in chunks
-                for i in range(2)
-            ],
-            0,
-        )
-        b = normed(h, gain_of(gm_v))
+    def states_of(c):
+        landed(r1.at[c], qh.at[c])
+        return [jnp.concatenate([h_all[c, i * cg + j].astype(F32) for j in range(cg)], 1) for i in range(2)]
+
+    def mlp(h):
+        b = normed(jnp.concatenate(h, 0), gain_of(gm_v))
         gate = dot(b, wg_v[...])
         up = dot(b, wu_v[...])
-        hidden = (jax.nn.silu(gate) * up).astype(BF16)
-        cut(dot(hidden, wd_v[...]), chunks, t2)
+        return dot((jax.nn.silu(gate) * up).astype(BF16), wd_v[...])
+
+    def spread_half(z, parts, buf, sems, phase):
+        for i in range(2):
+            axis = (i + phase) % 2
+            buf[z, i, my[axis]] = parts[i].astype(BF16)
+        for step in sorted(range(1, side), key=lambda k: -away[k]):
+            for i in range(2):
+                axis = (i + phase) % 2
+                there = lax.rem(my[axis] + step, side)
+                peer = there * side + my[1] if axis == 0 else my[0] * side + there
+                slot = buf.at[z, i, my[axis]]
+                send(slot, slot, (sems[0].at[z], sems[1].at[z]), peer)
+
+    def halves(term):
+        return term[:, : d // 2], term[:, d // 2 :]
+
+    def gathered(z, buf, sems):
+        landed(buf.at[z, :, 0 : side - 1], sems[1].at[z])
+        out = []
+        for i in range(2):
+            acc = buf[z, i, 0].astype(F32)
+            for k in range(1, side):
+                acc = acc + buf[z, i, k].astype(F32)
+            out.append(acc)
+        return out
+
+    def project_part(z):
+        s = steps - per + z * (per // 2)
+        seen = jnp.concatenate([seen_all[s + i] for i in range(per // 2)], 0).astype(BF16)
+        spread_half(z, halves(dot(seen, wo_v[...])), a1, (sa1, qa1), 0)
+
+    def states_part(z):
+        first = (chunks * rows) + z * small
+        h = x_v[first : first + small, :].astype(F32) + jnp.concatenate(gathered(z, b1, (sb1, qb1)), 1)
+        h_part[z] = h.astype(BF16)
+
+    def outputs_part(z):
+        y = h_part[z].astype(F32) + jnp.concatenate(gathered(z, b2, (sb2, qb2)), 1)
+        y_hbm[2 * chunks + z] = y.astype(BF16)
 
     def scatter2(c):
         scatter(t2.at[c], r2.at[c], (s2.at[c], q2.at[c]))
@@ -259,6 +294,10 @@
         @pl.when(lax.rem(s, per) == per - 1)
         def _():
             project(lax.div(s, per))
+
+        @pl.when(s == steps - per // 2 - 1)
+        def _():
+            project_part(0)
 
         @pl.when((s >= per) & (s < steps - per) & (lax.rem(s, per) == per - 2))
         def _():
@@ -278,24 +317,35 @@
         w = weights_of(s)
         values_in(s).wait()
         pv(s, w)
-    project(early)
-    states(early - 1)
+    project_part(1)
+    spread_half(0, gathered(0, a1, (sa1, qa1)), b1, (sb1, qb1), 1)
+    states(chunks - 1)
     first[4].wait()
     for i in range(1, len(weights)):
         weight(i).wait()
-    mlp(range(early - 1))
-    for c in range(early - 1):
+    cut(mlp([h for c in range(chunks - 1) for h in states_of(c)]), range(chunks - 1), t2)
+    spread_half(1, gathered(1, a1, (sa1, qa1)), b1, (sb1, qb1), 1)
+    for c in range(chunks - 1):
         scatter2(c)
-    states(early)
-    mlp([early - 1])
-    scatter2(early - 1)
-    outputs(0)
-    mlp([early])
-    scatter2(early)
-    for c in range(1, CHUNKS):
+    states_part(0)
+    term = mlp([*states_of(chunks - 1), h_part[0].astype(F32)])
+    cut(term[:rows], [chunks - 1], t2)
+    scatter2(chunks - 1)
+    spread_half(0, halves(term[rows:]), a2, (sa2, qa2), 0)
+    states_part(1)
+    spread_half(1, halves(mlp([h_part[1].astype(F32)])), a2, (sa2, qa2), 0)
+    for c in range(chunks - 1):
         outputs(c)
-
-    for c in range(CHUNKS):
+    spread_half(0, gathered(0, a2, (sa2, qa2)), b2, (sb2, qb2), 1)
+    outputs(chunks - 1)
+    spread_half(1, gathered(1, a2, (sa2, qa2)), b2, (sb2, qb2), 1)
+    outputs_part(0)
+    outputs_part(1)
+
+    for z in range(2):
+        for sem in (sa1, sb1, sa2, sb2):
+            landed(a1.at[z, :, 0 : side - 1], sem.at[z])
+    for c in range(chunks):
         landed(r1.at[c], s1.at[c])
         landed(r1.at[c], sh.at[c])
         landed(r1.at[c], s2.at[c])
@@ -312,7 +362,8 @@
         d, wide = wq.shape
         ff = w_gate.shape[1]
         fold = GROUP * wide
-        rows = batch // CHUNKS
+        rows = batch // QUARTER
+        chunks = QUARTER - 1
         block = (rows // 2, d // (n // 2))
         keys = jnp.transpose(k_cache, (0, 2, 3, 1)).reshape(batch * wide, cache)
         values = jnp.transpose(v_cache, (0, 2, 3, 1)).reshape(batch * wide, cache)
@@ -322,7 +373,7 @@
         turn = np.stack([np.tile([*cos, *cos], fold // head), np.tile([*-sin, *sin], fold // head)]).astype(np.float32)
         hbm = pl.BlockSpec(memory_space=pltpu.HBM)
         gains = (d // 128, 128)
-        dma, per_chunk = pltpu.SemaphoreType.DMA, pltpu.SemaphoreType.DMA((CHUNKS,))
+        dma, per_chunk = pltpu.SemaphoreType.DMA, pltpu.SemaphoreType.DMA((chunks,))
         return pl.pallas_call(
             functools.partial(kernel, n),
             out_shape=pltpu.VMEM((batch // block[0], block[0], d), BF16),
@@ -343,15 +394,17 @@
                 pltpu.VMEM((batch * heads, fold), F32),
                 pltpu.VMEM((LEAD + 1, GROUP * heads, cache), F32),
                 pltpu.VMEM((batch // GROUP, GROUP, wide), F32),
-                pltpu.VMEM((CHUNKS, *block), BF16),
-                pltpu.VMEM((CHUNKS, n, *block), BF16),
-                pltpu.VMEM((CHUNKS, n - 1, *block), BF16),
-                pltpu.VMEM((CHUNKS, n, *block), BF16),
-                pltpu.VMEM((CHUNKS, n, *block), BF16),
-                pltpu.VMEM((CHUNKS, n - 1, *block), BF16),
-                pltpu.VMEM((CHUNKS, *block), BF16),
+                pltpu.VMEM((chunks, *block), BF16),
+                pltpu.VMEM((chunks, n, *block), BF16),
+                pltpu.VMEM((chunks, n - 1, *block), BF16),
+                pltpu.VMEM((chunks, n, *block), BF16),
+                pltpu.VMEM((chunks, n, *block), BF16),
+                pltpu.VMEM((chunks, n - 1, *block), BF16),
+                pltpu.VMEM((chunks, *block), BF16),
+                *[pltpu.VMEM((2, 2, math.isqrt(n), rows // 2, d // 2), BF16)] * 4,
+                pltpu.VMEM((2, rows // 2, d), BF16),
                 dma((5,)), dma((4,)), dma((SLOTS,)), dma((SLOTS,)), per_chunk, per_chunk,
-                *[per_chunk] * 8,
+                *[per_chunk] * 8, *[dma((2,))] * 8,
             ],
             compiler_params=pltpu.CompilerParams(
                 collective_id=0, has_side_effects=True, vmem_limit_bytes=60 * 2**20

time: 59.6 us -> 59.7 us (level)
  no operation moved by 1% of the time
where the time goes in v4:
time: 59.7 us
  Pallas kernels  58.9 us (99%)
  local copies, waits for them, and re-layouts  0.75 us (1%)
    pallas_call x1, Pallas kernels, step(): pl.pallas_call(functools.partial(kernel, n), out_shape=pltpu.VMEM((batch...  58.9 us

profile of v4, /device:TPU:96, one launch (start us, length us, event | category | flops | bytes accessed | tf_op | source)
XLA Modules:
  0.0 59.7 jit_solution(18363260773220998885)
XLA Ops:
  0.0 58.9 %shard_map.109 = bf16[8,8,3072]{2,1,0:T(8,128)(2,1)S(1)} custom-call(bf16[64,3072]{1,0:T(8,128)(2,1)} %x_hbm.1, bf16[12288,2048]{1,0:T(8,128)(2,1)} %bitcast.11, bf16[12288,2048]{1,0:T(8,128)(2,1)} %bitcast.12, bf16[24,128]{1,0:T(8,128)(2,1)} %bitcast.14, bf16[192,3072]{1,0:T(8,128)(2,1)} %bitcast.13, bf16[192,3072]{1,0:T(8,128)(2,1)} %wo_hbm.1, ...), custom_call_target="tpu_custom_call" | custom-call | tf_op jit(solution)/shard_map/pallas_call | solution.py:377
  58.9 0.7 %copy.13 = bf16[64,3072]{1,0:T(8,128)(2,1)} copy(bf16[64,3072]{1,0:T(8,128)(2,1)S(1)} %bitcast.10) | data formatting | bytes 786432
